TPU v7x, 32 devices: a whole 2x2x4 slice. The times are simulated.
32 devices in a mesh: tm: 8 (over z, y), chan: 4 (over x, core).
Axes of the slice: x: 2, y: 2, z: 4, core: 2. Of those that a mesh axis runs over, the one named last changes fastest.
Arguments:
- coarse: bfloat16 [2, 24576, 4096], P(None, 'tm', 'chan'), may hold values from -6 to 6
- prototype: float32 [16, 1024], replicated, may hold values from -4 to 4
- req_block: int32 [4, 4], replicated, may hold values from 0 to 31, as said below
- req_start: int32 [4, 4], replicated, may hold values from 0 to 8, as said below
- req_frames: int32 [4, 4], replicated, may hold values from 1 to 9
- req_count: int32 [4], replicated, may hold values from 1 to 4, as said below
Outputs:
- spectra: bfloat16 [24, 4, 4, 2, 1024, 128], P('tm', 'chan')
Inputs may be any that keep to these rules, and one draw needn't show every extreme that they name: `req_block`: among the live slots of one owner at most 2 name blocks b with the same b // 8; in every draw some owner reaches 2. req_start + req_frames <= 9 in every slot; in every draw some live slot starts at hop 9 - 1 and some live slot spans all 9 frames. Slots q < req_count[c] of owner c are live, the others are empty; in every draw some owner has 4 live slots.
All inputs are finite; a program needn't handle non-finite values.
Results may differ from a plain program's by a relative error of at most 0.001.
Values may be sent and summed in bfloat16 or wider, within the bound.
A program may use at most 256 MiB of HBM per device.

v0:
```python
import math

import jax
import jax.numpy as jnp
from jax import lax
from jax.sharding import PartitionSpec as P

BLOCKW = 128
NFINE = 1024
TAPS = 16
HOPS_DEV = 3
MAXREQ = 4
PAIR = 2


def build_table():
    index_line = jnp.arange(NFINE, dtype=jnp.int32)
    products = index_line[:, None] * index_line[None, :] % NFINE
    angles = products.astype(jnp.float32) * (2.0 * math.pi / NFINE)
    cosine = jnp.cos(angles) / math.sqrt(NFINE)
    sine = jnp.sin(angles) / math.sqrt(NFINE)
    upper = jnp.concatenate([cosine, sine], axis=1)
    lower = jnp.concatenate([-sine, cosine], axis=1)
    return jnp.concatenate([upper, lower], axis=0)


def shards(coarse, prototype, req_block, req_start, req_frames, req_count):
    owners = lax.axis_size("chan")
    column = lax.axis_index("chan")
    row_index = lax.axis_index("tm")
    time_devices = lax.axis_size("tm")
    per_column = coarse.shape[2] // BLOCKW
    coarse_data = coarse.reshape(2, HOPS_DEV, NFINE, per_column, BLOCKW)
    slot_ids = jnp.arange(MAXREQ, dtype=jnp.int32)
    is_live = slot_ids[None, :] < req_count[:, None]
    sources = req_block // per_column
    is_mine = is_live & (sources == column)
    ranking = jnp.cumsum(is_mine.astype(jnp.int32), axis=1) - 1
    pair_ids = jnp.arange(PAIR, dtype=jnp.int32)
    picked = is_mine[:, None, :] & (ranking[:, None, :] == pair_ids[None, :, None])
    local_ids = req_block - column * per_column
    block_ids = jnp.arange(per_column, dtype=jnp.int32)
    matches = picked[:, :, :, None] & (
        local_ids[:, None, :, None] == block_ids[None, None, None, :]
    )
    chooser = jnp.any(matches, axis=2).astype(jnp.bfloat16)
    outgoing = jnp.einsum(
        "dpb,xhkbc->dpxhkc", chooser, coarse_data, preferred_element_type=jnp.float32
    ).astype(jnp.bfloat16)
    incoming = lax.all_to_all(outgoing, "chan", split_axis=0, concat_axis=0, tiled=True)
    owner_ids = jnp.arange(owners, dtype=jnp.int32)
    row_pick = owner_ids == column
    my_block = jnp.sum(jnp.where(row_pick[:, None], req_block, 0), axis=0)
    my_start = jnp.sum(jnp.where(row_pick[:, None], req_start, 0), axis=0)
    my_frames = jnp.sum(jnp.where(row_pick[:, None], req_frames, 0), axis=0)
    my_count = jnp.sum(jnp.where(row_pick, req_count, 0))
    my_live = slot_ids < my_count
    my_source = my_block // per_column
    earlier = (
        my_live[:, None]
        & my_live[None, :]
        & (my_source[:, None] == my_source[None, :])
        & (slot_ids[None, :] < slot_ids[:, None])
    )
    my_rank = jnp.sum(earlier.astype(jnp.int32), axis=1)
    arrival = my_source * PAIR + my_rank
    taker = (
        my_live[:, None] & (arrival[:, None] == jnp.arange(owners * PAIR, dtype=jnp.int32)[None, :])
    ).astype(jnp.bfloat16)
    arrived = incoming.reshape(owners * PAIR, 2, HOPS_DEV, NFINE, BLOCKW)
    slots = jnp.einsum(
        "qs,sxhkc->qxhkc", taker, arrived, preferred_element_type=jnp.float32
    ).astype(jnp.bfloat16)
    hop_ids = row_index * HOPS_DEV + jnp.arange(HOPS_DEV, dtype=jnp.int32)
    active = (
        my_live[:, None]
        & (hop_ids[None, :] >= my_start[:, None])
        & (hop_ids[None, :] < (my_start + my_frames)[:, None])
    )
    table = build_table()
    widest = MAXREQ * BLOCKW
    share = widest // time_devices
    all_hops = HOPS_DEV * time_devices
    sending = slots.transpose(2, 1, 3, 0, 4).reshape(HOPS_DEV, 2, NFINE, widest)
    gathered_cols = lax.all_to_all(sending, "tm", split_axis=3, concat_axis=0, tiled=True)
    padding = jnp.zeros((TAPS - 1, 2, NFINE, share), jnp.bfloat16)
    extended = jnp.concatenate([gathered_cols, padding], axis=0)
    col_filtered = jnp.zeros((all_hops, 2, NFINE, share), jnp.float32)
    for tap_index in range(TAPS):
        weights = prototype[tap_index][None, None, :, None]
        col_filtered = col_filtered + weights * extended[tap_index : tap_index + all_hops].astype(
            jnp.float32
        )
    flat = col_filtered.transpose(1, 2, 0, 3).reshape(2 * NFINE, all_hops * share)
    result = jnp.dot(
        table, flat, precision=lax.Precision.HIGHEST, preferred_element_type=jnp.float32
    )
    result = result.reshape(2, NFINE, all_hops, share).transpose(2, 0, 1, 3).astype(jnp.bfloat16)
    returned = lax.all_to_all(result, "tm", split_axis=0, concat_axis=3, tiled=True)
    spectra = returned.reshape(HOPS_DEV, 2, NFINE, MAXREQ, BLOCKW).transpose(0, 3, 1, 2, 4)
    keep = active.T[:, :, None, None, None]
    spectra = jnp.where(keep, spectra, jnp.zeros_like(spectra))
    return spectra[:, None]


def solution(mesh):
    return jax.shard_map(
        shards,
        mesh=mesh,
        in_specs=(P(None, "tm", "chan"), P(), P(), P(), P(), P()),
        out_specs=P("tm", "chan", None, None, None, None),
        check_vma=False,
    )
```

profile of v0, /device:TPU:5, one launch (start us, length us, event | category | flops | bytes accessed | tf_op | source)
XLA Modules:
  0.0 647.4 jit_solution(9923748060192311099)
XLA Ops:
  0.0 0.8 select_reduce_fusion.1
  0.9 0.8 fusion.23
  1.6 0.2 reduce_window_sum.11
  1.8 7.8 %copy.53 = bf16[768,8,8,128]{3,2,1,0:T(8,128)(2,1)S(1)} copy(bf16[768,8,8,128]{3,1,2,0:T(8,128)(2,1)} %bitcast.77) | data formatting | bytes 25165824
  9.6 0.1 and_reduce_fusion
  9.7 6.6 %convolution_convert_fusion = bf16[4,2,2,3,1024,128]{5,0,4,3,2,1:T(4,128)(2,1)} fusion(bf16[2,3,1024,8,128,1]{4,3,2,1,0,5:T(8,128)(2,1)S(1)} %bitcast.70, pred[4,2,8,1,1,1]{2,1,0,5,4,3:T(4,128)(4,1)S(1)} %bitcast.95), kind=kOutput, calls=%fused_computation.19 | convolution fusion | flops 106954752 | bytes 25165888 | tf_op jit(solution)/shard_map/dpb,xhkbc->dpxhkc/dot_general | solution.py:47
  16.3 11.6 %copy.38 = bf16[4,2,2,3,1024,128]{5,4,3,2,1,0:T(8,128)(2,1)} copy(bf16[4,2,2,3,1024,128]{5,0,4,3,2,1:T(4,128)(2,1)} %convolution_convert_fusion) | data formatting | bytes 25165824 | tf_op jit(solution)/shard_map/convert_element_type | solution.py:49
  27.9 7.1 %all-to-all-start = ((bf16[4,2,2,3,1024,128]{5,4,3,2,1,0:T(8,128)(2,1)}), bf16[4,2,2,3,1024,128]{5,4,3,2,1,0:T(8,128)(2,1)}, u32[]{:S(2)}, u32[]{:S(2)}) async-start(bf16[4,2,2,3,1024,128]{5,4,3,2,1,0:T(8,128)(2,1)} %copy.38), calls=%async_computation | async-start | bytes 25165824 | tf_op jit(solution)/shard_map/all_to_all | solution.py:50
  35.0 0.6 select_reduce_fusion.3
  35.6 0.6 iota_compare_fusion.5
  36.3 0.2 convert_reduce_fusion
  36.5 135.7 %all-to-all-done = bf16[4,2,2,3,1024,128]{5,4,3,2,1,0:T(8,128)(2,1)} async-done(((bf16[4,2,2,3,1024,128]{5,4,3,2,1,0:T(8,128)(2,1)}), bf16[4,2,2,3,1024,128]{5,4,3,2,1,0:T(8,128)(2,1)}, u32[]{:S(2)}, u32[]{:S(2)}) %all-to-all-start) | async-done | bytes 12582944 | tf_op jit(solution)/shard_map/all_to_all | solution.py:50
  172.1 14.5 %convert_bitcast_fusion.1 = bf16[3,2,1024,4,128]{4,3,2,0,1:T(4,128)(2,1)} fusion(bf16[8,2,3,1024,128]{4,3,2,1,0:T(8,128)(2,1)} %bitcast.7, s32[4]{0:T(128)S(1)} %multiply_add_fusion, pred[4]{0:T(512)(128)(4,1)S(1)} %iota_compare_fusion.5), kind=kOutput, calls=%fused_computation.23 | convolution fusion | flops 53477440 | bytes 18874388 | tf_op jit(solution)/shard_map/qs,sxhkc->qxhkc/dot_general | solution.py:71
  186.6 17.6 %copy.52 = bf16[3,2,1024,4,128]{2,1,0,4,3:T(2,128)(2,1)} copy(bf16[3,2,1024,4,128]{4,3,2,0,1:T(4,128)(2,1)} %convert_bitcast_fusion.1) | data formatting | bytes 12582912 | tf_op jit(solution)/shard_map/reshape | solution.py:84
  204.3 6.0 all-to-all-start.1
  210.3 15.8 %fusion.11 = f32[1024,1024]{1,0:T(8,128)S(1)} fusion(), kind=kLoop, calls=%fused_computation.35 | loop fusion | flops 16777216 | bytes 4194304 | tf_op jit(solution)/shard_map/neg | solution.py:23
  226.1 16.6 %sine_multiply_fusion = (f32[1024,1024]{1,0:T(8,128)S(1)}, f32[1024,1024]{1,0:T(8,128)S(1)}) fusion(), kind=kLoop, calls=%fused_computation.30 | loop fusion | flops 16777216 | bytes 8388608 | tf_op jit(solution)/shard_map/div | solution.py:21
  242.7 15.5 %maximum_maximum_fusion = f32[2048,2048]{1,0:T(8,128)} fusion(f32[1024,1024]{1,0:T(8,128)S(1)} %get-tuple-element.28, f32[1024,1024]{1,0:T(8,128)S(1)} %fusion.11, f32[1024,1024]{1,0:T(8,128)S(1)} %get-tuple-element.27), kind=kLoop, calls=%fused_computation.15 | loop fusion | flops 12582912 | bytes 29360128 | tf_op jit(solution)/shard_map/concatenate | solution.py:24
  258.2 89.4 %all-to-all-done.1 = bf16[3,2,1024,512]{2,1,0,3:T(2,128)(2,1)} async-done(((bf16[3,2,1024,512]{2,1,0,3:T(2,128)(2,1)}), bf16[3,2,1024,512]{2,1,0,3:T(2,128)(2,1)}, u32[]{:S(2)}, u32[]{:S(2)}) %all-to-all-start.1) | async-done | bytes 6291488 | tf_op jit(solution)/shard_map/all_to_all | solution.py:85
  347.6 4.8 copy.41
  352.3 1.2 copy.42
  353.6 21.7 %add_bitcast_fusion = f32[2,1024,24,64]{1,3,0,2:T(8,128)S(1)} fusion(bf16[24,2,1024,64]{2,3,1,0:T(8,128)(2,1)S(1)} %bitcast.75, f32[1024]{0:T(1024)S(1)} %bitcast.93, f32[1024]{0:T(1024)S(1)} %bitcast.94, f32[1024]{0:T(1024)S(1)} %bitcast.80, f32[1024]{0:T(1024)S(1)} %bitcast.81, f32[1024]{0:T(1024)S(1)} %bitcast.82, f32[1024]{0:T(1024)S(1)} %bitcast.83, ...), kind=kLoop, calls=%fused_computation.18 | loop fusion | flops 147849216 | bytes 18939904 | tf_op jit(solution)/shard_map/transpose | solution.py:94
  375.3 11.1 %copy.43 = f32[2,1024,24,64]{1,0,3,2:T(2,128)} copy(f32[2,1024,24,64]{1,3,0,2:T(8,128)S(1)} %add_bitcast_fusion) | data formatting | bytes 25165824 | tf_op jit(solution)/shard_map/transpose | solution.py:94
  386.5 15.4 %copy.54 = f32[192,8,2,1024]{3,1,2,0:T(8,128)} copy(f32[192,8,2,1024]{3,2,1,0:T(2,128)} %bitcast.71) | data formatting | bytes 25165824
  401.9 84.4 %convert_bitcast_fusion = bf16[24,2,1024,64]{2,3,0,1:T(8,128)(2,1)S(1)} fusion(f32[2,1024,2048,1]{2,1,3,0:T(8,128)} %bitcast.76, f32[24,64,2048,1]{2,1,0,3:T(8,128)} %bitcast.78), kind=kOutput, calls=%fused_computation.22 | convolution fusion | flops 77312557056 | bytes 35651584 | tf_op jit(solution)/shard_map/dot_general | solution.py:95
  486.3 3.4 copy.44
  489.7 4.7 all-to-all-start.2
  494.4 0.1 compare_and_fusion.1
  494.5 137.2 %all-to-all-done.2 = bf16[24,2,1024,64]{2,3,1,0:T(8,128)(2,1)} async-done(((bf16[24,2,1024,64]{2,3,1,0:T(8,128)(2,1)}), bf16[24,2,1024,64]{2,3,1,0:T(8,128)(2,1)}, u32[]{:S(2)}, u32[]{:S(2)}) %all-to-all-start.2) | async-done | bytes 6291488 | tf_op jit(solution)/shard_map/all_to_all | solution.py:99
  631.7 3.5 copy.45
  635.2 3.1 fusion.2
  638.4 8.6 %copy.46 = bf16[3,1,4,2,1024,128]{5,4,3,2,1,0:T(8,128)(2,1)} copy(bf16[3,1,4,2,1024,128]{4,5,2,3,0,1:T(8,128)(2,1)} %fusion.2) | data formatting | bytes 12582912 | tf_op jit(solution)/shard_map/broadcast_in_dim | solution.py:103
  (13 shorter events, 0.2 us)
Async XLA Ops:
  27.9 7.1 %copy-start.1 = (s32[4]{0:T(128)S(1)}, s32[4]{0:T(128)}, u32[]{:S(2)}) copy-start(s32[4]{0:T(128)} %param.11) | copy-start | bytes 52
  27.9 144.3 %all-to-all-start = ((bf16[4,2,2,3,1024,128]{5,4,3,2,1,0:T(8,128)(2,1)}), bf16[4,2,2,3,1024,128]{5,4,3,2,1,0:T(8,128)(2,1)}, u32[]{:S(2)}, u32[]{:S(2)}) async-start(bf16[4,2,2,3,1024,128]{5,4,3,2,1,0:T(8,128)(2,1)} %copy.38), calls=%async_computation | async-start | bytes 25165824 | tf_op jit(solution)/shard_map/all_to_all | solution.py:50
  186.6 23.6 %copy-start = (f32[16,1024]{1,0:T(8,128)S(1)}, f32[16,1024]{1,0:T(8,128)}, u32[]{:S(2)}) copy-start(f32[16,1024]{1,0:T(8,128)} %param.7) | copy-start | bytes 196612
  204.3 143.3 %all-to-all-start.1 = ((bf16[3,2,1024,512]{2,1,0,3:T(2,128)(2,1)}), bf16[3,2,1024,512]{2,1,0,3:T(2,128)(2,1)}, u32[]{:S(2)}, u32[]{:S(2)}) async-start(bf16[3,2,1024,512]{2,1,0,3:T(2,128)(2,1)} %bitcast.72), calls=%async_computation.1 | async-start | bytes 12582912 | tf_op jit(solution)/shard_map/all_to_all | solution.py:85
  489.7 142.0 %all-to-all-start.2 = ((bf16[24,2,1024,64]{2,3,1,0:T(8,128)(2,1)}), bf16[24,2,1024,64]{2,3,1,0:T(8,128)(2,1)}, u32[]{:S(2)}, u32[]{:S(2)}) async-start(bf16[24,2,1024,64]{2,3,1,0:T(8,128)(2,1)} %copy.44), calls=%async_computation.2 | async-start | bytes 12582912 | tf_op jit(solution)/shard_map/all_to_all | solution.py:99
where the time goes:
time: 658 us; the launch traced here: 647 us
  waiting for transfers between devices  362 us (55%)
  matrix products  105 us (16%)
  local copies, waits for them, and re-layouts  85.1 us (13%)
  other arithmetic  76.2 us (12%)
  starting transfers between devices  17.8 us (3%)
    all_to_all x1, waiting for transfers between devices, shards(): lax.all_to_all(result, 'tm', split_axis=0, concat_axis=3, tiled=True)  137 us
    all_to_all x1, waiting for transfers between devices, shards(): lax.all_to_all(outgoing, 'chan', split_axis=0, concat_axis=0, tiled=True)  136 us
    all_to_all x1, waiting for transfers between devices, shards(): lax.all_to_all(sending, 'tm', split_axis=3, concat_axis=0, tiled=True)  89.4 us
    dot_general x1, matrix products, shards(): jnp.dot(table, flat, precision=lax.Precision.HIGHEST, preferred_element_t...  84.4 us
    unnamed x6, local copies, waits for them, and re-layouts  23.2 us
    transpose x1, other arithmetic, shards(): col_filtered.transpose(1, 2, 0, 3).reshape(2 * NFINE, all_hops * share)  21.7 us
    reshape x1, local copies, waits for them, and re-layouts, shards(): sending = slots.transpose(2, 1, 3, 0, 4).reshape(HOPS_DEV, 2, NFINE, widest)  17.6 us
    div x1, other arithmetic, build_table(): sine = jnp.sin(angles) / math.sqrt(NFINE)  16.6 us
  transfers between devices with their start and end apart: 3, of which 3 were waited for; matrix products, arithmetic and copies ran while one was open for 8% of the time, Pallas kernels for 0%

commit v1 on v0

v1 whole, which is shorter than its diff:
```python
import functools
import math

import jax
import jax.numpy as jnp
import numpy as np
from jax import lax
from jax.experimental import pallas as pl
from jax.experimental.pallas import tpu as pltpu
from jax.sharding import PartitionSpec as P

BLOCKW = 128
NFINE = 1024
TAPS = 16
MAXREQ = 4
PAIR = 2
CHUNKS = 3
ANY = pl.BlockSpec(memory_space=pl.ANY)


def build_table():
    line = jnp.arange(NFINE, dtype=jnp.int32)
    products = line[:, None] * line[None, :] % NFINE
    angles = products.astype(jnp.float32) * (2.0 * math.pi / NFINE)
    scale = 1.0 / math.sqrt(NFINE)
    return jnp.concatenate([jnp.cos(angles) * scale, jnp.sin(angles) * scale], axis=0)


def pack_kernel(chosen, coarse_ref, out_ref):
    out_ref[...] = coarse_ref[...].reshape(out_ref.shape)


def pack(coarse, chosen, first, hops):
    count = chosen.shape[0]
    return pl.pallas_call(
        pack_kernel,
        out_shape=jax.ShapeDtypeStruct((count, 2, hops * NFINE, BLOCKW), coarse.dtype),
        grid_spec=pltpu.PrefetchScalarGridSpec(
            num_scalar_prefetch=1,
            grid=(count,),
            in_specs=[pl.BlockSpec((2, hops * NFINE, BLOCKW), lambda i, c: (0, first, c[i]))],
            out_specs=pl.BlockSpec((1, 2, hops * NFINE, BLOCKW), lambda i, c: (i, 0, 0, 0)),
        ),
        cost_estimate=pl.CostEstimate(
            flops=0, transcendentals=0, bytes_accessed=count * 8 * hops * NFINE * BLOCKW
        ),
    )(chosen, coarse)


def select_kernel(pieces, arrival, in_ref, out_ref):
    share = BLOCKW // pieces
    for piece in range(pieces):
        cols = slice(piece * share, (piece + 1) * share)
        out_ref[piece] = jnp.concatenate([in_ref[0, 0, :, cols], in_ref[0, 1, :, cols]], axis=-1)


def select(incoming, arrival, pieces, hops):
    width = 2 * BLOCKW // pieces
    rows = hops * NFINE
    return pl.pallas_call(
        functools.partial(select_kernel, pieces),
        out_shape=jax.ShapeDtypeStruct((MAXREQ * pieces, rows, width), incoming.dtype),
        grid_spec=pltpu.PrefetchScalarGridSpec(
            num_scalar_prefetch=1,
            grid=(MAXREQ, hops),
            in_specs=[pl.BlockSpec((1, 2, NFINE, BLOCKW), lambda q, h, a: (a[q], 0, h, 0))],
            out_specs=pl.BlockSpec((pieces, NFINE, width), lambda q, h, a: (q, h, 0)),
        ),
        cost_estimate=pl.CostEstimate(
            flops=0, transcendentals=0, bytes_accessed=MAXREQ * 8 * rows * BLOCKW
        ),
    )(arrival, incoming)


def return_kernel(size, keepers, hops, res_ref, out_ref, send_sems, recv_sems):
    me = lax.axis_index("tm")
    barrier = pltpu.get_barrier_semaphore()

    @pl.loop(1, size)
    def _(step):
        other = lax.rem(me + step, size)
        pl.semaphore_signal(barrier, inc=1, device_id={"tm": other})

    pl.semaphore_wait(barrier, size - 1)

    def copy(step):
        target = lax.rem(me + step, size)
        return pltpu.make_async_remote_copy(
            src_ref=res_ref.at[pl.ds(target * hops, hops)],
            dst_ref=out_ref.at[me],
            send_sem=send_sems.at[step],
            recv_sem=recv_sems.at[step],
            device_id={"tm": target},
        )

    def arriving(step):
        source = lax.rem(me + size - step, size)
        return pltpu.make_async_remote_copy(
            src_ref=res_ref.at[pl.ds(0, hops)],
            dst_ref=out_ref.at[source],
            send_sem=send_sems.at[step],
            recv_sem=recv_sems.at[step],
            device_id={"tm": source},
        )

    @pl.loop(1, size)
    def _(step):
        @pl.when(lax.rem(me + step, size) < keepers)
        def _():
            copy(step).start()

    @pl.when(me < keepers)
    def _():
        @pl.loop(1, size)
        def _(step):
            arriving(step).wait_recv()

    @pl.loop(1, size)
    def _(step):
        @pl.when(lax.rem(me + step, size) < keepers)
        def _():
            copy(step).wait_send()


def give_back(result, size, keepers, hops):
    shape = (size, hops) + result.shape[1:]
    return pl.pallas_call(
        functools.partial(return_kernel, size, keepers, hops),
        out_shape=jax.ShapeDtypeStruct(shape, result.dtype),
        in_specs=[ANY],
        out_specs=ANY,
        scratch_shapes=[pltpu.SemaphoreType.DMA((size,)), pltpu.SemaphoreType.DMA((size,))],
        compiler_params=pltpu.CompilerParams(collective_id=0, has_side_effects=True),
    )(result)


def final_kernel(pieces, meta, got_ref, own_ref, out_ref):
    share = BLOCKW // pieces
    slot, hop = pl.program_id(0), pl.program_id(1)
    row = meta[0]
    active = meta[2 + slot * pl.num_programs(1) + hop] > 0

    @pl.when(jnp.logical_not(active))
    def _():
        out_ref[...] = jnp.zeros_like(out_ref)

    @pl.when(active)
    def _():
        data = [
            jnp.where(slot * pieces + piece == row, own_ref[0], got_ref[piece, 0])
            for piece in range(pieces)
        ]
        for part in range(2):
            cols = slice(part * share, (part + 1) * share)
            out_ref[0, 0, part] = jnp.concatenate([d[:, cols] for d in data], axis=-1)


def assemble(got, result, active, row, keepers, pieces):
    size, hops, _, width = got.shape
    base = jnp.minimum(row, keepers - 1) * hops
    meta = jnp.concatenate(
        [jnp.stack([row, base]).astype(jnp.int32), active.astype(jnp.int32).reshape(-1)]
    )
    return pl.pallas_call(
        functools.partial(final_kernel, pieces),
        out_shape=jax.ShapeDtypeStruct((hops, MAXREQ, 2, NFINE, BLOCKW), got.dtype),
        grid_spec=pltpu.PrefetchScalarGridSpec(
            num_scalar_prefetch=1,
            grid=(MAXREQ, hops),
            in_specs=[
                pl.BlockSpec((pieces, 1, NFINE, width), lambda q, h, m: (q, h, 0, 0)),
                pl.BlockSpec((1, NFINE, width), lambda q, h, m: (m[1] + h, 0, 0)),
            ],
            out_specs=pl.BlockSpec((1, 1, 2, NFINE, BLOCKW), lambda q, h, m: (h, q, 0, 0, 0)),
        ),
    )(meta, got, result)


def shards(coarse, prototype, req_block, req_start, req_frames, req_count):
    owners = lax.axis_size("chan")
    column = lax.axis_index("chan")
    row = lax.axis_index("tm")
    size = lax.axis_size("tm")
    per_column = coarse.shape[2] // BLOCKW
    hops = coarse.shape[1] // NFINE
    all_hops = hops * size
    frames = all_hops - TAPS + 1
    keepers = -(-frames // hops)
    pieces = size // MAXREQ
    width = 2 * BLOCKW // pieces
    share = BLOCKW // pieces

    slot_ids = jnp.arange(MAXREQ, dtype=jnp.int32)
    live = slot_ids[None, :] < req_count[:, None]
    sources = req_block // per_column
    same = (
        live[:, :, None]
        & live[:, None, :]
        & (sources[:, :, None] == sources[:, None, :])
        & (slot_ids[None, None, :] < slot_ids[None, :, None])
    )
    rank = jnp.sum(same.astype(jnp.int32), axis=2)
    picked = (
        (live & (sources == column))[:, None, :]
        & (rank[:, None, :] == jnp.arange(PAIR, dtype=jnp.int32)[None, :, None])
    )
    local = req_block - column * per_column
    chosen = jnp.sum(jnp.where(picked, local[:, None, :], 0), axis=2).reshape(-1)
    chosen = jnp.clip(chosen, 0, per_column - 1).astype(jnp.int32)
    mine = (jnp.arange(owners, dtype=jnp.int32) == column)[:, None]

    def own(table):
        return jnp.sum(jnp.where(mine, table, 0), axis=0)

    my_live = slot_ids < own(req_count[:, None])[0]
    arrival = jnp.where(my_live, own(sources) * PAIR + own(rank), 0)
    arrival = jnp.clip(arrival, 0, owners * PAIR - 1).astype(jnp.int32)
    my_start, my_frames = own(req_start), own(req_frames)
    hop_ids = row * hops + jnp.arange(hops, dtype=jnp.int32)
    active = (
        my_live[:, None]
        & (hop_ids[None, :] >= my_start[:, None])
        & (hop_ids[None, :] < (my_start + my_frames)[:, None])
    )

    table = build_table()
    chunks = CHUNKS if hops % CHUNKS == 0 else 1
    per_chunk = hops // chunks
    parts = []
    for chunk in range(chunks):
        outgoing = pack(coarse, chosen, chunk, per_chunk)
        incoming = lax.all_to_all(outgoing, "chan", split_axis=0, concat_axis=0, tiled=True)
        sending = select(incoming, arrival, pieces, per_chunk)
        gathered = lax.all_to_all(sending, "tm", split_axis=0, concat_axis=0, tiled=True)
        parts.append(gathered.reshape(size, per_chunk, NFINE, width))
    samples = [
        parts[(h % hops) // per_chunk][h // hops, (h % hops) % per_chunk] for h in range(all_hops)
    ]
    filtered = []
    for frame in range(frames):
        total = None
        for tap in range(TAPS):
            term = prototype[tap][:, None] * samples[frame + tap].astype(jnp.float32)
            total = term if total is None else total + term
        filtered.append(total)
    flat = jnp.concatenate(filtered, axis=1)
    both = jnp.dot(table, flat, precision=lax.Precision.HIGH, preferred_element_type=jnp.float32)
    both = both.reshape(2, NFINE, frames, 2, share)
    cosine, sine = both[0], both[1]
    result = jnp.stack(
        [cosine[:, :, 0] + sine[:, :, 1], cosine[:, :, 1] - sine[:, :, 0]], axis=2
    ).astype(jnp.bfloat16)
    result = result.reshape(NFINE, frames, width).transpose(1, 0, 2)
    extra = keepers * hops - frames
    if extra:
        result = jnp.concatenate([result, jnp.zeros((extra, NFINE, width), result.dtype)], axis=0)
    got = give_back(result, size, keepers, hops)
    return assemble(got, result, active, row, keepers, pieces)[:, None]


def solution(mesh):
    return jax.shard_map(
        shards,
        mesh=mesh,
        in_specs=(P(None, "tm", "chan"), P(), P(), P(), P(), P()),
        out_specs=P("tm", "chan", None, None, None, None),
        check_vma=False,
    )
```

time: 658 us -> 515 us (0.78); the launches traced: 647 us -> 512 us
  Pallas kernels: 0 us -> 150 us
  waiting for transfers between devices: 362 us -> 236 us
  matrix products: 105 us -> 18.7 us
  local copies, waits for them, and re-layouts: 85.1 us -> 9.99 us
  starting transfers between devices: 17.8 us -> 32.3 us
  other arithmetic: 76.2 us -> 65 us
    pallas_call x0 -> x8, Pallas kernels: none -> 150 us  [the longest x1 106 us: give_back(): pl.pallas_call(functools.partial(return_kernel, size, keepers, hops), out...]
    all_to_all x2 -> x3, waiting for transfers between devices: 227 us -> 114 us  [shards(): lax.all_to_all(sending, 'tm', split_axis=0, concat_axis=0, tiled=True)]
    dot_general x3 -> x1, matrix products: 105 us -> 18.7 us  [shards(): jnp.dot(table, flat, precision=lax.Precision.HIGH, preferred_element_type...]
    unnamed x0 -> x8, other arithmetic: none -> 34.8 us
    unnamed x6 -> x12, local copies, waits for them, and re-layouts: 23.2 us -> 0.03 us
    transpose x1 -> x0, other arithmetic: 21.7 us -> none  [shards(): col_filtered.transpose(1, 2, 0, 3).reshape(2 * NFINE, all_hops * share)]
    mul x0 -> x1, other arithmetic: none -> 17.8 us  [build_table(): jnp.sin(angles) * scale]
    reshape x1 -> x0, local copies, waits for them, and re-layouts: 17.6 us -> none  [shards(): sending = slots.transpose(2, 1, 3, 0, 4).reshape(HOPS_DEV, 2, NFINE, widest)]
  transfers between devices with their start and end apart: 3 -> 6, of which waited for: 3 -> 6; matrix products, arithmetic and copies ran while one was open for 8% -> 4% of each run, Pallas kernels for 0% -> 5%
where the time goes in v1:
time: 515 us; the launch traced here: 512 us
  waiting for transfers between devices  236 us (46%)
  Pallas kernels  150 us (29%)
  other arithmetic  65 us (13%)
  starting transfers between devices  32.3 us (6%)
  matrix products  18.7 us (4%)
  local copies, waits for them, and re-layouts  9.99 us (2%)
    all_to_all x3, waiting for transfers between devices, shards(): lax.all_to_all(outgoing, 'chan', split_axis=0, concat_axis=0, tiled=True)  122 us
    all_to_all x3, waiting for transfers between devices, shards(): lax.all_to_all(sending, 'tm', split_axis=0, concat_axis=0, tiled=True)  114 us
    pallas_call x1, Pallas kernels, give_back(): pl.pallas_call(functools.partial(return_kernel, size, keepers, hops), out...  106 us
    unnamed x8, other arithmetic  34.8 us
    dot_general x1, matrix products, shards(): jnp.dot(table, flat, precision=lax.Precision.HIGH, preferred_element_type...  18.7 us
    pallas_call x3, Pallas kernels, pack(): pl.pallas_call(pack_kernel, out_shape=jax.ShapeDtypeStruct((count, 2, hop...  18.5 us
    mul x1, other arithmetic, build_table(): jnp.sin(angles) * scale  17.8 us
    all_to_all x3, starting transfers between devices, shards(): lax.all_to_all(outgoing, 'chan', split_axis=0, concat_axis=0, tiled=True)  17.4 us
  transfers between devices with their start and end apart: 6, of which 6 were waited for; matrix products, arithmetic and copies ran while one was open for 4% of the time, Pallas kernels for 5%

profile of v1, /device:TPU:5, one launch (start us, length us, event | category | flops | bytes accessed | tf_op | source)
XLA Modules:
  0.0 512.2 jit_solution(17501764025239905603)
XLA Ops:
  2.6 6.2 %shard_map.68 = bf16[8,2,1024,128]{3,2,1,0:T(8,128)(2,1)} custom-call(s32[8]{0:T(128)} %min.26.chosen, bf16[2,3072,1024]{2,1,0:T(8,128)(2,1)} %coarse_ref.5), custom_call_target="tpu_custom_call" | custom-call | bytes 8388608 | tf_op jit(solution)/shard_map/pallas_call | solution.py:35
  8.7 5.5 %all-to-all-start.4 = ((bf16[8,2,1024,128]{3,2,1,0:T(8,128)(2,1)}), bf16[8,2,1024,128]{3,2,1,0:T(8,128)(2,1)}, u32[]{:S(2)}, u32[]{:S(2)}) async-start(bf16[8,2,1024,128]{3,2,1,0:T(8,128)(2,1)} %shard_map.68), calls=%async_computation.4 | async-start | bytes 8388608 | tf_op jit(solution)/shard_map/all_to_all | solution.py:232
  14.2 6.2 %shard_map.66 = bf16[8,2,1024,128]{3,2,1,0:T(8,128)(2,1)} custom-call(s32[8]{0:T(128)} %min.26.chosen, bf16[2,3072,1024]{2,1,0:T(8,128)(2,1)} %coarse_ref.5), custom_call_target="tpu_custom_call" | custom-call | bytes 8388608 | tf_op jit(solution)/shard_map/pallas_call | solution.py:35
  20.4 40.8 %all-to-all-done.4.in_ref = bf16[8,2,1024,128]{3,2,1,0:T(8,128)(2,1)} async-done(((bf16[8,2,1024,128]{3,2,1,0:T(8,128)(2,1)}), bf16[8,2,1024,128]{3,2,1,0:T(8,128)(2,1)}, u32[]{:S(2)}, u32[]{:S(2)}) %all-to-all-start.4) | async-done | bytes 4194336 | tf_op jit(solution)/shard_map/all_to_all | solution.py:232
  61.2 6.2 %all-to-all-start.2 = ((bf16[8,2,1024,128]{3,2,1,0:T(8,128)(2,1)}), bf16[8,2,1024,128]{3,2,1,0:T(8,128)(2,1)}, u32[]{:S(2)}, u32[]{:S(2)}) async-start(bf16[8,2,1024,128]{3,2,1,0:T(8,128)(2,1)} %shard_map.66), calls=%async_computation.2 | async-start | bytes 8388608 | tf_op jit(solution)/shard_map/all_to_all | solution.py:232
  67.3 6.2 %shard_map.64 = bf16[8,2,1024,128]{3,2,1,0:T(8,128)(2,1)} custom-call(s32[8]{0:T(128)} %min.26.chosen, bf16[2,3072,1024]{2,1,0:T(8,128)(2,1)} %coarse_ref.5), custom_call_target="tpu_custom_call" | custom-call | bytes 8388608 | tf_op jit(solution)/shard_map/pallas_call | solution.py:35
  73.5 41.1 %all-to-all-done.2.in_ref = bf16[8,2,1024,128]{3,2,1,0:T(8,128)(2,1)} async-done(((bf16[8,2,1024,128]{3,2,1,0:T(8,128)(2,1)}), bf16[8,2,1024,128]{3,2,1,0:T(8,128)(2,1)}, u32[]{:S(2)}, u32[]{:S(2)}) %all-to-all-start.2) | async-done | bytes 4194336 | tf_op jit(solution)/shard_map/all_to_all | solution.py:232
  114.6 5.8 %all-to-all-start = ((bf16[8,2,1024,128]{3,2,1,0:T(8,128)(2,1)}), bf16[8,2,1024,128]{3,2,1,0:T(8,128)(2,1)}, u32[]{:S(2)}, u32[]{:S(2)}) async-start(bf16[8,2,1024,128]{3,2,1,0:T(8,128)(2,1)} %shard_map.64), calls=%async_computation | async-start | bytes 8388608 | tf_op jit(solution)/shard_map/all_to_all | solution.py:232
  122.5 4.8 shard_map.69
  127.3 40.4 %all-to-all-done.in_ref = bf16[8,2,1024,128]{3,2,1,0:T(8,128)(2,1)} async-done(((bf16[8,2,1024,128]{3,2,1,0:T(8,128)(2,1)}), bf16[8,2,1024,128]{3,2,1,0:T(8,128)(2,1)}, u32[]{:S(2)}, u32[]{:S(2)}) %all-to-all-start) | async-done | bytes 4194336 | tf_op jit(solution)/shard_map/all_to_all | solution.py:232
  167.7 5.8 %all-to-all-start.5 = ((bf16[8,1024,128]{2,1,0:T(8,128)(2,1)}), bf16[8,1024,128]{2,1,0:T(8,128)(2,1)S(1)}, u32[]{:S(2)}, u32[]{:S(2)}) async-start(bf16[8,1024,128]{2,1,0:T(8,128)(2,1)} %shard_map.69), calls=%async_computation.5 | async-start | bytes 4194304 | tf_op jit(solution)/shard_map/all_to_all | solution.py:234
  173.4 4.8 shard_map.67
  178.2 42.7 %all-to-all-done.5 = bf16[8,1024,128]{2,1,0:T(8,128)(2,1)S(1)} async-done(((bf16[8,1024,128]{2,1,0:T(8,128)(2,1)}), bf16[8,1024,128]{2,1,0:T(8,128)(2,1)S(1)}, u32[]{:S(2)}, u32[]{:S(2)}) %all-to-all-start.5) | async-done | bytes 2097184 | tf_op jit(solution)/shard_map/all_to_all | solution.py:234
  221.0 4.5 all-to-all-start.3
  225.5 5.0 shard_map.65
  230.5 42.7 %all-to-all-done.3 = bf16[8,1024,128]{2,1,0:T(8,128)(2,1)} async-done(((bf16[8,1024,128]{2,1,0:T(8,128)(2,1)}), bf16[8,1024,128]{2,1,0:T(8,128)(2,1)}, u32[]{:S(2)}, u32[]{:S(2)}) %all-to-all-start.3) | async-done | bytes 2097184 | tf_op jit(solution)/shard_map/all_to_all | solution.py:234
  273.1 4.5 all-to-all-start.1
  279.2 17.8 %sine_multiply_fusion = (f32[1024,1024]{1,0:T(8,128)}, f32[1024,1024]{1,0:T(8,128)}) fusion(), kind=kLoop, calls=%fused_computation.10 | loop fusion | flops 16777216 | bytes 8388608 | tf_op jit(solution)/shard_map/mul | solution.py:26
  297.0 28.3 %all-to-all-done.1 = bf16[8,1024,128]{2,1,0:T(8,128)(2,1)} async-done(((bf16[8,1024,128]{2,1,0:T(8,128)(2,1)}), bf16[8,1024,128]{2,1,0:T(8,128)(2,1)}, u32[]{:S(2)}, u32[]{:S(2)}) %all-to-all-start.1) | async-done | bytes 2097184 | tf_op jit(solution)/shard_map/all_to_all | solution.py:234
  325.3 4.2 fusion.27
  329.5 4.3 fusion.43
  333.8 4.2 fusion.64
  338.0 4.2 fusion.84
  342.3 4.2 fusion.105
  346.5 4.2 fusion.86
  350.7 4.2 fusion.66
  355.0 5.1 %fusion.45 = f32[1024,1152]{1,0:T(8,128)S(1)} fusion(f32[1024,1152]{1,0:T(8,128)S(1)} %fusion.66, f32[1024]{0:T(1024)S(1)} %bitcast.524, f32[1024]{0:T(1024)S(1)} %bitcast.533, f32[1024]{0:T(1024)S(1)} %bitcast.407, f32[1024]{0:T(1024)S(1)} %bitcast.416, f32[1024]{0:T(1024)S(1)} %bitcast.425, f32[1024]{0:T(1024)S(1)} %bitcast.434, f32[1024]{0:T(1024)S(1)} %bitcast.443, ...), kind=kLoop, calls=%fused_computation.195 | loop fusion | flops 6160384 | bytes 4784128
  364.4 18.7 %fusion = f32[2048,1152]{0,1:T(8,128)} fusion(f32[1024,1152]{1,0:T(8,128)S(1)} %fusion.48, f32[1024,1024]{1,0:T(8,128)S(1)} %copy-done, f32[1024,1024]{1,0:T(8,128)S(1)} %copy-done.1), kind=kOutput, calls=%fused_computation | convolution fusion | flops 14497611776 | bytes 22544384 | tf_op jit(solution)/shard_map/dot_general | solution.py:247
  383.1 4.8 fusion.160
  390.8 4.3 copy.15
  395.2 106.0 %shard_map.70.got_ref = bf16[8,3,1024,128]{3,2,1,0:T(8,128)(2,1)} custom-call(bf16[9,1024,128]{2,1,0:T(8,128)(2,1)} %bitcast.386), custom_call_target="tpu_custom_call" | custom-call | tf_op jit(solution)/shard_map/pallas_call | solution.py:127
  501.2 11.1 %shard_map.71 = bf16[3,4,2,1024,128]{4,3,2,1,0:T(8,128)(2,1)} custom-call(s32[14]{0:T(128)} %pad_add_fusion.meta, bf16[8,3,1024,128]{3,2,1,0:T(8,128)(2,1)} %shard_map.70.got_ref, bf16[9,1024,128]{2,1,0:T(8,128)(2,1)} %bitcast.387), custom_call_target="tpu_custom_call" | custom-call | tf_op jit(solution)/shard_map/pallas_call | solution.py:164
  (33 shorter events, 13.4 us)
Async XLA Ops:
  8.7 52.4 %all-to-all-start.4 = ((bf16[8,2,1024,128]{3,2,1,0:T(8,128)(2,1)}), bf16[8,2,1024,128]{3,2,1,0:T(8,128)(2,1)}, u32[]{:S(2)}, u32[]{:S(2)}) async-start(bf16[8,2,1024,128]{3,2,1,0:T(8,128)(2,1)} %shard_map.68), calls=%async_computation.4 | async-start | bytes 8388608 | tf_op jit(solution)/shard_map/all_to_all | solution.py:232
  61.2 53.4 %all-to-all-start.2 = ((bf16[8,2,1024,128]{3,2,1,0:T(8,128)(2,1)}), bf16[8,2,1024,128]{3,2,1,0:T(8,128)(2,1)}, u32[]{:S(2)}, u32[]{:S(2)}) async-start(bf16[8,2,1024,128]{3,2,1,0:T(8,128)(2,1)} %shard_map.66), calls=%async_computation.2 | async-start | bytes 8388608 | tf_op jit(solution)/shard_map/all_to_all | solution.py:232
  73.5 46.9 %copy-start.5 = (s32[4]{0:T(128)S(1)}, s32[4]{0:T(128)}, u32[]{:S(2)}) copy-start(s32[4]{0:T(128)} %param.11) | copy-start | bytes 52
  73.5 47.6 %copy-start.3 = (s32[4,4]{1,0:T(4,128)S(1)}, s32[4,4]{1,0:T(4,128)}, u32[]{:S(2)}) copy-start(s32[4,4]{1,0:T(4,128)} %param.9) | copy-start | bytes 196
  73.5 47.6 %copy-start.4 = (s32[4,4]{1,0:T(4,128)S(1)}, s32[4,4]{1,0:T(4,128)}, u32[]{:S(2)}) copy-start(s32[4,4]{1,0:T(4,128)} %param.10) | copy-start | bytes 196
  114.6 53.0 %all-to-all-start = ((bf16[8,2,1024,128]{3,2,1,0:T(8,128)(2,1)}), bf16[8,2,1024,128]{3,2,1,0:T(8,128)(2,1)}, u32[]{:S(2)}, u32[]{:S(2)}) async-start(bf16[8,2,1024,128]{3,2,1,0:T(8,128)(2,1)} %shard_map.64), calls=%async_computation | async-start | bytes 8388608 | tf_op jit(solution)/shard_map/all_to_all | solution.py:232
  167.7 53.3 %all-to-all-start.5 = ((bf16[8,1024,128]{2,1,0:T(8,128)(2,1)}), bf16[8,1024,128]{2,1,0:T(8,128)(2,1)S(1)}, u32[]{:S(2)}, u32[]{:S(2)}) async-start(bf16[8,1024,128]{2,1,0:T(8,128)(2,1)} %shard_map.69), calls=%async_computation.5 | async-start | bytes 4194304 | tf_op jit(solution)/shard_map/all_to_all | solution.py:234
  221.0 52.2 %all-to-all-start.3 = ((bf16[8,1024,128]{2,1,0:T(8,128)(2,1)}), bf16[8,1024,128]{2,1,0:T(8,128)(2,1)}, u32[]{:S(2)}, u32[]{:S(2)}) async-start(bf16[8,1024,128]{2,1,0:T(8,128)(2,1)} %shard_map.67), calls=%async_computation.3 | async-start | bytes 4194304 | tf_op jit(solution)/shard_map/all_to_all | solution.py:234
  225.5 53.7 %copy-start.2 = (f32[16,1024]{1,0:T(8,128)S(1)}, f32[16,1024]{1,0:T(8,128)}, u32[]{:S(2)}) copy-start(f32[16,1024]{1,0:T(8,128)} %param.7) | copy-start | bytes 196612
  273.1 52.2 %all-to-all-start.1 = ((bf16[8,1024,128]{2,1,0:T(8,128)(2,1)}), bf16[8,1024,128]{2,1,0:T(8,128)(2,1)}, u32[]{:S(2)}, u32[]{:S(2)}) async-start(bf16[8,1024,128]{2,1,0:T(8,128)(2,1)} %shard_map.65), calls=%async_computation.1 | async-start | bytes 4194304 | tf_op jit(solution)/shard_map/all_to_all | solution.py:234
  355.0 9.4 %copy-start = (f32[1024,1024]{1,0:T(8,128)S(1)}, f32[1024,1024]{1,0:T(8,128)}, u32[]{:S(2)}) copy-start(f32[1024,1024]{1,0:T(8,128)} %get-tuple-element.33) | copy-start | bytes 12582916
  355.0 9.4 %copy-start.1 = (f32[1024,1024]{1,0:T(8,128)S(1)}, f32[1024,1024]{1,0:T(8,128)}, u32[]{:S(2)}) copy-start(f32[1024,1024]{1,0:T(8,128)} %get-tuple-element.34) | copy-start | bytes 12582916

commit v2 on v1

--- a/solution.py
+++ b/solution.py
@@ -3,7 +3,6 @@
 
 import jax
 import jax.numpy as jnp
-import numpy as np
 from jax import lax
 from jax.experimental import pallas as pl
 from jax.experimental.pallas import tpu as pltpu
@@ -14,7 +13,8 @@
 TAPS = 16
 MAXREQ = 4
 PAIR = 2
-CHUNKS = 3
+ROWS = 128
+STEP = 16
 ANY = pl.BlockSpec(memory_space=pl.ANY)
 
 
@@ -70,6 +70,161 @@
             flops=0, transcendentals=0, bytes_accessed=MAXREQ * 8 * rows * BLOCKW
         ),
     )(arrival, incoming)
+
+
+def exchange_kernel(
+    owners, size, a_in, b_in, a_out, b_out, a_tmp, b_tmp, a_send, a_recv, b_send, b_recv, local
+):
+    column, row = lax.axis_index("chan"), lax.axis_index("tm")
+    barrier = pltpu.get_barrier_semaphore()
+
+    @pl.loop(1, owners)
+    def _(step):
+        other = lax.rem(column + step, owners)
+        pl.semaphore_signal(barrier, inc=1, device_id={"chan": other})
+
+    @pl.loop(1, size)
+    def _(step):
+        other = lax.rem(row + step, size)
+        pl.semaphore_signal(barrier, inc=1, device_id={"tm": other})
+
+    pl.semaphore_wait(barrier, owners + size - 2)
+
+    def a_copy(step, source, target, device):
+        return pltpu.make_async_remote_copy(
+            src_ref=a_in.at[pl.ds(target * PAIR, PAIR)],
+            dst_ref=a_out.at[pl.ds(source * PAIR, PAIR)],
+            send_sem=a_send.at[step],
+            recv_sem=a_recv.at[step],
+            device_id={"chan": device},
+        )
+
+    def b_copy(step, source, target, device):
+        return pltpu.make_async_remote_copy(
+            src_ref=b_in.at[target],
+            dst_ref=b_out.at[source],
+            send_sem=b_send.at[step],
+            recv_sem=b_recv.at[step],
+            device_id={"tm": device},
+        )
+
+    @pl.loop(1, size)
+    def _(step):
+        target = lax.rem(row + step, size)
+        b_copy(step, row, target, target).start()
+
+    @pl.loop(1, owners)
+    def _(step):
+        target = lax.rem(column + step, owners)
+        a_copy(step, column, target, target).start()
+
+    a_read = pltpu.make_async_copy(a_in.at[pl.ds(column * PAIR, PAIR)], a_tmp, local.at[0])
+    b_read = pltpu.make_async_copy(b_in.at[row], b_tmp, local.at[1])
+    a_read.start()
+    b_read.start()
+    a_read.wait()
+    b_read.wait()
+    a_write = pltpu.make_async_copy(a_tmp, a_out.at[pl.ds(column * PAIR, PAIR)], local.at[2])
+    b_write = pltpu.make_async_copy(b_tmp, b_out.at[row], local.at[3])
+    a_write.start()
+    b_write.start()
+    a_write.wait()
+    b_write.wait()
+
+    @pl.loop(1, owners)
+    def _(step):
+        source = lax.rem(column + owners - step, owners)
+        copy = a_copy(step, source, column, source)
+        copy.wait_recv()
+        copy.wait_send()
+
+    @pl.loop(1, size)
+    def _(step):
+        source = lax.rem(row + size - step, size)
+        copy = b_copy(step, source, row, source)
+        copy.wait_recv()
+        copy.wait_send()
+
+
+def exchange(outgoing, sending, owners, size, collective):
+    sem = pltpu.SemaphoreType.DMA
+    return pl.pallas_call(
+        functools.partial(exchange_kernel, owners, size),
+        out_shape=(
+            jax.ShapeDtypeStruct(outgoing.shape, outgoing.dtype),
+            jax.ShapeDtypeStruct(sending.shape, sending.dtype),
+        ),
+        in_specs=[ANY, ANY],
+        out_specs=(ANY, ANY),
+        scratch_shapes=[
+            pltpu.VMEM((PAIR,) + outgoing.shape[1:], outgoing.dtype),
+            pltpu.VMEM(sending.shape[1:], sending.dtype),
+            sem((owners,)),
+            sem((owners,)),
+            sem((size,)),
+            sem((size,)),
+            sem((4,)),
+        ],
+        compiler_params=pltpu.CompilerParams(collective_id=collective, has_side_effects=True),
+    )(outgoing, sending)
+
+
+def filter_kernel(hops, frames, weights_ref, *refs):
+    out_ref = refs[-1]
+    width = refs[0].shape[-1]
+
+    @pl.loop(0, ROWS // STEP)
+    def _(step):
+        rows = pl.ds(pl.multiple_of(step * STEP, STEP), STEP)
+        weights = [
+            jnp.broadcast_to(weights_ref[rows, tap : tap + 1], (STEP, width)) for tap in range(TAPS)
+        ]
+        for frame in range(frames):
+            total = None
+            for tap in range(TAPS):
+                hop = frame + tap
+                term = weights[tap] * refs[hop % hops][hop // hops, rows, :].astype(jnp.float32)
+                total = term if total is None else total + term
+            out_ref[rows, frame * width : (frame + 1) * width] = total
+
+
+def polyphase(parts, prototype, frames):
+    hops = len(parts)
+    size, _, width = parts[0].shape
+    return pl.pallas_call(
+        functools.partial(filter_kernel, hops, frames),
+        out_shape=jax.ShapeDtypeStruct((NFINE, frames * width), jnp.float32),
+        grid=(NFINE // ROWS,),
+        in_specs=[pl.BlockSpec((ROWS, TAPS), lambda i: (i, 0))]
+        + [pl.BlockSpec((size, ROWS, width), lambda i: (0, i, 0))] * hops,
+        out_specs=pl.BlockSpec((ROWS, frames * width), lambda i: (i, 0)),
+    )(prototype.T, *parts)
+
+
+def combine_kernel(frames, share, both_ref, out_ref):
+    frame = pl.program_id(0)
+
+    @pl.when(frame < frames)
+    def _():
+        sine = both_ref[1]
+        turned = jnp.concatenate([sine[:, share:], -sine[:, :share]], axis=-1)
+        out_ref[0] = (both_ref[0] + turned).astype(out_ref.dtype)
+
+    @pl.when(frame >= frames)
+    def _():
+        out_ref[...] = jnp.zeros_like(out_ref)
+
+
+def combine(both, frames, padded, width):
+    return pl.pallas_call(
+        functools.partial(combine_kernel, frames, width // 2),
+        out_shape=jax.ShapeDtypeStruct((padded, NFINE, width), jnp.bfloat16),
+        grid=(padded,),
+        in_specs=[
+            pl.BlockSpec((2, NFINE, width), lambda f: (0, 0, jnp.minimum(f, frames - 1))),
+        ],
+        out_specs=pl.BlockSpec((1, NFINE, width), lambda f: (f, 0, 0)),
+    )(both)
 
 
 def return_kernel(size, keepers, hops, res_ref, out_ref, send_sems, recv_sems):
@@ -224,36 +379,30 @@
     )
 
     table = build_table()
-    chunks = CHUNKS if hops % CHUNKS == 0 else 1
-    per_chunk = hops // chunks
+    outgoing = [pack(coarse, chosen, hop, 1) for hop in range(hops)]
+    incoming = lax.all_to_all(outgoing[0], "chan", split_axis=0, concat_axis=0, tiled=True)
     parts = []
-    for chunk in range(chunks):
-        outgoing = pack(coarse, chosen, chunk, per_chunk)
-        incoming = lax.all_to_all(outgoing, "chan", split_axis=0, concat_axis=0, tiled=True)
-        sending = select(incoming, arrival, pieces, per_chunk)
-        gathered = lax.all_to_all(sending, "tm", split_axis=0, concat_axis=0, tiled=True)
-        parts.append(gathered.reshape(size, per_chunk, NFINE, width))
-    samples = [
-        parts[(h % hops) // per_chunk][h // hops, (h % hops) % per_chunk] for h in range(all_hops)
-    ]
-    filtered = []
-    for frame in range(frames):
-        total = None
-        for tap in range(TAPS):
-            term = prototype[tap][:, None] * samples[frame + tap].astype(jnp.float32)
-            total = term if total is None else total + term
-        filtered.append(total)
-    flat = jnp.concatenate(filtered, axis=1)
+    for hop in range(1, hops):
+        sending = select(incoming, arrival, pieces, 1)
+        incoming, gathered = exchange(outgoing[hop], sending, owners, size, hop)
+        parts.append(gathered)
+    sending = select(incoming, arrival, pieces, 1)
+    parts.append(lax.all_to_all(sending, "tm", split_axis=0, concat_axis=0, tiled=True))
+    flat = polyphase(parts, prototype, frames)
     both = jnp.dot(table, flat, precision=lax.Precision.HIGH, preferred_element_type=jnp.float32)
-    both = both.reshape(2, NFINE, frames, 2, share)
-    cosine, sine = both[0], both[1]
-    result = jnp.stack(
-        [cosine[:, :, 0] + sine[:, :, 1], cosine[:, :, 1] - sine[:, :, 0]], axis=2
-    ).astype(jnp.bfloat16)
-    result = result.reshape(NFINE, frames, width).transpose(1, 0, 2)
-    extra = keepers * hops - frames
-    if extra:
-        result = jnp.concatenate([result, jnp.zeros((extra, NFINE, width), result.dtype)], axis=0)
+    padded = keepers * hops
+    if width % 128 == 0:
+        result = combine(both.reshape(2, NFINE, frames * width), frames, padded, width)
+    else:
+        both = both.reshape(2, NFINE, frames, 2, share)
+        cosine, sine = both[0], both[1]
+        result = jnp.stack(
+            [cosine[:, :, 0] + sine[:, :, 1], cosine[:, :, 1] - sine[:, :, 0]], axis=2
+        ).astype(jnp.bfloat16)
+        result = result.reshape(NFINE, frames, width).transpose(1, 0, 2)
+        if padded > frames:
+            zeros = jnp.zeros((padded - frames, NFINE, width), result.dtype)
+            result = jnp.concatenate([result, zeros], axis=0)
     got = give_back(result, size, keepers, hops)
     return assemble(got, result, active, row, keepers, pieces)[:, None]
 

time: 515 us -> 392 us (0.76)
  waiting for transfers between devices: 236 us -> 60.7 us
  Pallas kernels: 150 us -> 269 us
  other arithmetic: 65 us -> 22.9 us
  starting transfers between devices: 32.3 us -> 10.8 us
  local copies, waits for them, and re-layouts: 9.99 us -> 3.18 us
    pallas_call x0 -> x4, Pallas kernels: none -> 121 us  [the longest x2 99.3 us: exchange(): pl.pallas_call(functools.partial(exchange_kernel, owners, size), out_shap...]
    all_to_all x3 -> x1, waiting for transfers between devices: 122 us -> 33.5 us  [shards(): lax.all_to_all(outgoing[0], 'chan', split_axis=0, concat_axis=0, tiled=True)]
    all_to_all x3 -> x1, waiting for transfers between devices: 114 us -> 27.3 us  [shards(): lax.all_to_all(sending, 'tm', split_axis=0, concat_axis=0, tiled=True)]
    unnamed x8 -> x0, other arithmetic: 34.8 us -> none
    all_to_all x3 -> x1, starting transfers between devices: 17.4 us -> 4.87 us  [shards(): lax.all_to_all(outgoing[0], 'chan', split_axis=0, concat_axis=0, tiled=True)]
    all_to_all x3 -> x1, starting transfers between devices: 14.9 us -> 5.9 us  [shards(): lax.all_to_all(sending, 'tm', split_axis=0, concat_axis=0, tiled=True)]
  transfers between devices with their start and end apart: 6 -> 2, of which waited for: 6 -> 2; matrix products, arithmetic and copies ran while one was open for 4% -> 6% of each run, Pallas kernels for 5% -> 3%
where the time goes in v2:
time: 392 us; the launch traced here: 389 us
  Pallas kernels  269 us (69%)
  waiting for transfers between devices  60.7 us (15%)
  other arithmetic  22.9 us (6%)
  matrix products  22.6 us (6%)
  starting transfers between devices  10.8 us (3%)
    pallas_call x1, Pallas kernels, give_back(): pl.pallas_call(functools.partial(return_kernel, size, keepers, hops), out...  106 us
    pallas_call x2, Pallas kernels, exchange(): pl.pallas_call(functools.partial(exchange_kernel, owners, size), out_shap...  99.3 us
    all_to_all x1, waiting for transfers between devices, shards(): lax.all_to_all(outgoing[0], 'chan', split_axis=0, concat_axis=0, tiled=True)  33.5 us
    all_to_all x1, waiting for transfers between devices, shards(): lax.all_to_all(sending, 'tm', split_axis=0, concat_axis=0, tiled=True)  27.3 us
    dot_general x1, matrix products, shards(): jnp.dot(table, flat, precision=lax.Precision.HIGH, preferred_element_type...  22.6 us
    pallas_call x3, Pallas kernels, pack(): pl.pallas_call(pack_kernel, out_shape=jax.ShapeDtypeStruct((count, 2, hop...  18.8 us
    mul x1, other arithmetic, build_table(): jnp.sin(angles) * scale  17.8 us
    pallas_call x1, Pallas kernels, polyphase(): pl.pallas_call(functools.partial(filter_kernel, hops, frames), out_shape=...  12.1 us
  transfers between devices with their start and end apart: 2, of which 2 were waited for; matrix products, arithmetic and copies ran while one was open for 6% of the time, Pallas kernels for 3%

profile of v2, /device:TPU:5, one launch (start us, length us, event | category | flops | bytes accessed | tf_op | source)
XLA Modules:
  0.0 388.9 jit_solution(9844782129556199454)
XLA Ops:
  0.0 0.7 broadcast_subtract_fusion
  0.7 0.8 compare_and_fusion
  1.5 0.2 convert_reduce_fusion
  1.7 0.1 select_reduce_fusion
  1.8 0.1 copy.12
  1.9 0.6 min.24.chosen
  2.6 6.3 %shard_map.65 = bf16[8,2,1024,128]{3,2,1,0:T(8,128)(2,1)} custom-call(s32[8]{0:T(128)} %min.24.chosen, bf16[2,3072,1024]{2,1,0:T(8,128)(2,1)} %coarse_ref.5), custom_call_target="tpu_custom_call" | custom-call | bytes 8388608 | tf_op jit(solution)/shard_map/pallas_call | solution.py:35
  8.8 4.9 %all-to-all-start = ((bf16[8,2,1024,128]{3,2,1,0:T(8,128)(2,1)}), bf16[8,2,1024,128]{3,2,1,0:T(8,128)(2,1)}, u32[]{:S(2)}, u32[]{:S(2)}) async-start(bf16[8,2,1024,128]{3,2,1,0:T(8,128)(2,1)} %shard_map.65), calls=%async_computation | async-start | bytes 8388608 | tf_op jit(solution)/shard_map/all_to_all | solution.py:383
  13.7 6.2 %shard_map.68.a_in = bf16[8,2,1024,128]{3,2,1,0:T(8,128)(2,1)} custom-call(s32[8]{0:T(128)} %min.24.chosen, bf16[2,3072,1024]{2,1,0:T(8,128)(2,1)} %coarse_ref.5), custom_call_target="tpu_custom_call" | custom-call | bytes 8388608 | tf_op jit(solution)/shard_map/pallas_call | solution.py:35
  19.9 6.3 %shard_map.64.a_in = bf16[8,2,1024,128]{3,2,1,0:T(8,128)(2,1)} custom-call(s32[8]{0:T(128)} %min.24.chosen, bf16[2,3072,1024]{2,1,0:T(8,128)(2,1)} %coarse_ref.5), custom_call_target="tpu_custom_call" | custom-call | bytes 8388608 | tf_op jit(solution)/shard_map/pallas_call | solution.py:35
  26.3 0.7 select_reduce_fusion.5
  26.9 0.1 select_reduce_fusion.2
  27.0 1.2 select_clamp_fusion.arrival
  28.2 33.5 %all-to-all-done.in_ref = bf16[8,2,1024,128]{3,2,1,0:T(8,128)(2,1)} async-done(((bf16[8,2,1024,128]{3,2,1,0:T(8,128)(2,1)}), bf16[8,2,1024,128]{3,2,1,0:T(8,128)(2,1)}, u32[]{:S(2)}, u32[]{:S(2)}) %all-to-all-start) | async-done | bytes 4194336 | tf_op jit(solution)/shard_map/all_to_all | solution.py:383
  61.7 4.0 %shard_map.66.b_in = bf16[8,1024,128]{2,1,0:T(8,128)(2,1)} custom-call(s32[4]{0:T(128)} %select_clamp_fusion.arrival, bf16[8,2,1024,128]{3,2,1,0:T(8,128)(2,1)} %all-to-all-done.in_ref), custom_call_target="tpu_custom_call" | custom-call | bytes 4194304 | tf_op jit(solution)/shard_map/pallas_call | solution.py:60
  65.7 49.6 %shard_map.67 = (bf16[8,2,1024,128]{3,2,1,0:T(8,128)(2,1)}, bf16[8,1024,128]{2,1,0:T(8,128)(2,1)}) custom-call(bf16[8,2,1024,128]{3,2,1,0:T(8,128)(2,1)} %shard_map.64.a_in, bf16[8,1024,128]{2,1,0:T(8,128)(2,1)} %shard_map.66.b_in), custom_call_target="tpu_custom_call" | custom-call | tf_op jit(solution)/shard_map/pallas_call | solution.py:151
  115.3 3.9 %shard_map.69.b_in = bf16[8,1024,128]{2,1,0:T(8,128)(2,1)} custom-call(s32[4]{0:T(128)} %select_clamp_fusion.arrival, bf16[8,2,1024,128]{3,2,1,0:T(8,128)(2,1)} %get-tuple-element.10.in_ref), custom_call_target="tpu_custom_call" | custom-call | bytes 4194304 | tf_op jit(solution)/shard_map/pallas_call | solution.py:60
  119.3 49.7 %shard_map.70 = (bf16[8,2,1024,128]{3,2,1,0:T(8,128)(2,1)}, bf16[8,1024,128]{2,1,0:T(8,128)(2,1)}) custom-call(bf16[8,2,1024,128]{3,2,1,0:T(8,128)(2,1)} %shard_map.68.a_in, bf16[8,1024,128]{2,1,0:T(8,128)(2,1)} %shard_map.69.b_in), custom_call_target="tpu_custom_call" | custom-call | tf_op jit(solution)/shard_map/pallas_call | solution.py:151
  168.9 4.1 %shard_map.71 = bf16[8,1024,128]{2,1,0:T(8,128)(2,1)} custom-call(s32[4]{0:T(128)} %select_clamp_fusion.arrival, bf16[8,2,1024,128]{3,2,1,0:T(8,128)(2,1)} %get-tuple-element.12.in_ref), custom_call_target="tpu_custom_call" | custom-call | bytes 4194304 | tf_op jit(solution)/shard_map/pallas_call | solution.py:60
  173.0 5.9 %all-to-all-start.1 = ((bf16[8,1024,128]{2,1,0:T(8,128)(2,1)}), bf16[8,1024,128]{2,1,0:T(8,128)(2,1)S(1)}, u32[]{:S(2)}, u32[]{:S(2)}) async-start(bf16[8,1024,128]{2,1,0:T(8,128)(2,1)} %shard_map.71), calls=%async_computation.1 | async-start | bytes 4194304 | tf_op jit(solution)/shard_map/all_to_all | solution.py:390
  178.9 0.6 iota_compare_fusion.4
  179.6 0.1 reshape.96
  179.7 1.0 copy.11
  180.7 0.7 pad_add_fusion.meta
  181.4 17.8 %sine_multiply_fusion = (f32[1024,1024]{1,0:T(8,128)}, f32[1024,1024]{1,0:T(8,128)}) fusion(), kind=kLoop, calls=%fused_computation.10 | loop fusion | flops 16777216 | bytes 8388608 | tf_op jit(solution)/shard_map/mul | solution.py:26
  199.2 27.3 %all-to-all-done.1.refs_2_ = bf16[8,1024,128]{2,1,0:T(8,128)(2,1)S(1)} async-done(((bf16[8,1024,128]{2,1,0:T(8,128)(2,1)}), bf16[8,1024,128]{2,1,0:T(8,128)(2,1)S(1)}, u32[]{:S(2)}, u32[]{:S(2)}) %all-to-all-start.1) | async-done | bytes 2097184 | tf_op jit(solution)/shard_map/all_to_all | solution.py:390
  226.4 1.3 copy-done
  227.8 12.1 %shard_map.72 = f32[1024,1152]{1,0:T(8,128)} custom-call(f32[1024,16]{1,0:T(8,128)} %bitcast.9, bf16[8,1024,128]{2,1,0:T(8,128)(2,1)} %get-tuple-element.9.refs_0_, bf16[8,1024,128]{2,1,0:T(8,128)(2,1)} %get-tuple-element.11.refs_1_, bf16[8,1024,128]{2,1,0:T(8,128)(2,1)} %copy-done), custom_call_target="tpu_custom_call" | custom-call | tf_op jit(solution)/shard_map/pallas_call | solution.py:194
  239.9 22.6 %fusion = f32[2048,1152]{1,0:T(8,128)} fusion(f32[1024,1152]{1,0:T(8,128)} %shard_map.72, f32[1024,1024]{1,0:T(8,128)} %get-tuple-element.21, f32[1024,1024]{1,0:T(8,128)} %get-tuple-element.22), kind=kOutput, calls=%fused_computation | convolution fusion | flops 14497611776 | bytes 22544384 | tf_op jit(solution)/shard_map/dot_general | solution.py:392
  262.5 9.2 %shard_map.73.res_ref.own_ref = bf16[9,1024,128]{2,1,0:T(8,128)(2,1)} custom-call(f32[2,1024,1152]{2,1,0:T(8,128)} %bitcast.8), custom_call_target="tpu_custom_call" | custom-call | tf_op jit(solution)/shard_map/pallas_call | solution.py:219
  271.7 106.0 %shard_map.74.got_ref = bf16[8,3,1024,128]{3,2,1,0:T(8,128)(2,1)} custom-call(bf16[9,1024,128]{2,1,0:T(8,128)(2,1)} %shard_map.73.res_ref.own_ref), custom_call_target="tpu_custom_call" | custom-call | tf_op jit(solution)/shard_map/pallas_call | solution.py:282
  377.7 11.1 %shard_map.75 = bf16[3,4,2,1024,128]{4,3,2,1,0:T(8,128)(2,1)} custom-call(s32[14]{0:T(128)} %pad_add_fusion.meta, bf16[8,3,1024,128]{3,2,1,0:T(8,128)(2,1)} %shard_map.74.got_ref, bf16[9,1024,128]{2,1,0:T(8,128)(2,1)} %shard_map.73.res_ref.own_ref), custom_call_target="tpu_custom_call" | custom-call | tf_op jit(solution)/shard_map/pallas_call | solution.py:319
  (14 shorter events, 0.1 us)
Async XLA Ops:
  8.8 52.8 %all-to-all-start = ((bf16[8,2,1024,128]{3,2,1,0:T(8,128)(2,1)}), bf16[8,2,1024,128]{3,2,1,0:T(8,128)(2,1)}, u32[]{:S(2)}, u32[]{:S(2)}) async-start(bf16[8,2,1024,128]{3,2,1,0:T(8,128)(2,1)} %shard_map.65), calls=%async_computation | async-start | bytes 8388608 | tf_op jit(solution)/shard_map/all_to_all | solution.py:383
  19.9 6.3 %copy-start.4 = (s32[4]{0:T(128)S(1)}, s32[4]{0:T(128)}, u32[]{:S(2)}) copy-start(s32[4]{0:T(128)} %param.11) | copy-start | bytes 52
  19.9 7.0 %copy-start.2 = (s32[4,4]{1,0:T(4,128)S(1)}, s32[4,4]{1,0:T(4,128)}, u32[]{:S(2)}) copy-start(s32[4,4]{1,0:T(4,128)} %param.9) | copy-start | bytes 196
  19.9 7.0 %copy-start.3 = (s32[4,4]{1,0:T(4,128)S(1)}, s32[4,4]{1,0:T(4,128)}, u32[]{:S(2)}) copy-start(s32[4,4]{1,0:T(4,128)} %param.10) | copy-start | bytes 196
  168.9 10.8 %copy-start.1 = (f32[16,1024]{1,0:T(8,128)S(1)}, f32[16,1024]{1,0:T(8,128)}, u32[]{:S(2)}) copy-start(f32[16,1024]{1,0:T(8,128)} %param.7) | copy-start | bytes 196612
  173.0 53.4 %all-to-all-start.1 = ((bf16[8,1024,128]{2,1,0:T(8,128)(2,1)}), bf16[8,1024,128]{2,1,0:T(8,128)(2,1)S(1)}, u32[]{:S(2)}, u32[]{:S(2)}) async-start(bf16[8,1024,128]{2,1,0:T(8,128)(2,1)} %shard_map.71), calls=%async_computation.1 | async-start | bytes 4194304 | tf_op jit(solution)/shard_map/all_to_all | solution.py:390
  226.4 1.4 copy-start
